TPU v7x, 32 devices: a whole 2x2x4 slice. The times are simulated.
32 devices in a mesh: row: 8 (over z, y), col: 4 (over x, core).
Axes of the slice: x: 2, y: 2, z: 4, core: 2. Of those that a mesh axis runs over, the one named last changes fastest.
Arguments:
- moment: bfloat16 [2, 4096, 4096], P(None, 'row', 'col'), may hold values from -6 to 6
- second: float32 [2, 4096, 4096], P(None, 'row', 'col'), may hold values from 0.04 to 2
- left_old: bfloat16 [2, 4096, 4096], P(None, 'col', 'row'), may hold values from -0.09375 to 0.09375
- left_new: bfloat16 [2, 4096, 4096], P(None, 'col', 'row'), may hold values from -0.09375 to 0.09375
- right_old: bfloat16 [4096, 4096], P('row', 'col'), may hold values from -0.09375 to 0.09375
- right_new: bfloat16 [4096, 4096], P('row', 'col'), may hold values from -0.09375 to 0.09375
Outputs:
- moment_new: bfloat16 [2, 4096, 4096], P(None, 'row', 'col')
- direction: bfloat16 [2, 4096, 4096], P(None, 'row', 'col')
All inputs are finite; a program needn't handle non-finite values.
Results may differ from a plain program's by a relative error of at most 0.03.
Values may be sent and summed in bfloat16 or wider, within the bound.
A program may use at most 128 MiB of HBM per device.

v0:
```python
import jax
import jax.numpy as jnp
from jax import lax
from jax.sharding import PartitionSpec as P


def fold_stacked(left_panel, incoming):
    return jnp.einsum("bij,bjk->bik", left_panel, incoming, preferred_element_type=jnp.float32)


def fold_right(right_panel, incoming):
    return jnp.einsum("bik,qk->biq", incoming, right_panel, preferred_element_type=jnp.float32)


def local(moment, second, left_old, left_new, right_old, right_new):
    old_right_rows = lax.all_gather(right_old, "col", axis=1, tiled=True)
    right_terms = jnp.dot(right_new.T, old_right_rows, preferred_element_type=jnp.float32)
    right_panel = lax.psum(right_terms.astype(jnp.bfloat16), "row")
    old_rows = lax.all_gather(left_old, "row", axis=2, tiled=True)
    left_terms = jnp.einsum("bwi,bwj->bij", left_new, old_rows, preferred_element_type=jnp.float32)
    left_panel = lax.psum(left_terms.astype(jnp.bfloat16), "col")
    summed = fold_stacked(left_panel, lax.all_gather(moment, "row", axis=1, tiled=True))
    rotated = summed.astype(jnp.bfloat16)
    result = fold_right(right_panel, lax.all_gather(rotated, "col", axis=2, tiled=True))
    moment_new = result.astype(jnp.bfloat16)
    direction = (moment_new.astype(jnp.float32) / (jnp.sqrt(second) + 1e-08)).astype(jnp.bfloat16)
    return (moment_new, direction)


def solution(mesh):
    return jax.shard_map(
        local,
        mesh=mesh,
        in_specs=(
            P(None, "row", "col"),
            P(None, "row", "col"),
            P(None, "col", "row"),
            P(None, "col", "row"),
            P("row", "col"),
            P("row", "col"),
        ),
        out_specs=(P(None, "row", "col"), P(None, "row", "col")),
        check_vma=False,
    )
```

profile of v0, /device:TPU:0, one launch (start us, length us, event | category | flops | bytes accessed | tf_op | source)
XLA Modules:
  0.0 1013.9 jit_solution(3959504421610417472)
XLA Ops:
  7.2 0.0 copy-start
  7.2 0.0 all-gather.5.cloned.1.call-start
  7.2 0.7 all-gather.5.cloned.1.call-update
  7.9 0.0 all-gather.11.cloned.1.call-start
  8.0 0.7 all-gather.11.cloned.1.call-update
  8.7 0.0 all-gather.7.cloned.1.call-start
  8.7 0.7 all-gather.7.cloned.1.call-update
  9.4 0.0 all-reduce.3.cloned.1.call-start
  9.4 230.6 %all-gather.5.cloned.1.call-done = bf16[2,1024,4096]{2,1,0:T(8,128)(2,1)} async-done(((bf16[2,1024,512]{2,1,0:T(8,128)(2,1)}), bf16[2,1024,4096]{2,1,0:T(8,128)(2,1)}) %all-gather.5.cloned.1.call-update) | async-done | bytes 16777232 | tf_op jit(solution)/shard_map/all_gather | solution.py:19
  240.1 0.0 copy-done
  240.1 17.1 %convolution_convert_fusion.1 = bf16[2,512,4096]{2,1,0:T(8,128)(2,1)} fusion(bf16[2,1024,512]{2,1,0:T(8,128)(2,1)S(1)} %copy-done, bf16[2,1024,4096]{2,1,0:T(8,128)(2,1)} %all-gather.5.cloned.1.call-done), kind=kOutput, calls=%fused_computation.3 | convolution fusion | flops 8594128896 | bytes 27262976 | tf_op jit(solution)/shard_map/bwi,bwj->bij/dot_general | solution.py:20
  257.2 0.0 copy-start.2
  257.2 0.0 all-reduce.3.cloned.1.call-update
  257.2 0.0 all-reduce.5.cloned.1.call-start
  257.2 17.1 %all-gather.11.cloned.1.call-done = bf16[512,4096]{1,0:T(8,128)(2,1)} async-done(((bf16[512,1024]{1,0:T(8,128)(2,1)}), bf16[512,4096]{1,0:T(8,128)(2,1)}) %all-gather.11.cloned.1.call-update) | async-done | bytes 4194320 | tf_op jit(solution)/shard_map/all_gather | solution.py:16
  274.3 0.0 copy-done.2
  274.3 8.9 convolution_convert_fusion
  283.3 0.0 all-reduce.5.cloned.1.call-update
  283.3 0.2 all-gather.9.cloned.1.call-start
  283.5 220.3 %all-gather.7.cloned.1.call-done = bf16[2,4096,1024]{2,1,0:T(8,128)(2,1)} async-done(((bf16[2,512,1024]{2,1,0:T(8,128)(2,1)}), bf16[2,4096,1024]{2,1,0:T(8,128)(2,1)}) %all-gather.7.cloned.1.call-update) | async-done | bytes 16777232 | tf_op jit(solution)/shard_map/all_gather | solution.py:22
  503.8 153.4 %all-reduce.3.cloned.1.call-done = bf16[2,512,4096]{2,1,0:T(8,128)(2,1)} async-done(((bf16[2,512,4096]{2,1,0:T(8,128)(2,1)}), bf16[2,512,4096]{2,1,0:T(8,128)(2,1)}) %all-reduce.3.cloned.1.call-update) | async-done | bytes 8388624 | tf_op jit(solution)/shard_map/psum | solution.py:21
  657.2 15.8 %convolution_convert_fusion.2 = bf16[2,512,1024]{2,1,0:T(8,128)(2,1)} fusion(bf16[2,512,4096]{2,1,0:T(8,128)(2,1)} %all-reduce.3.cloned.1.call-done, bf16[2,4096,1024]{2,1,0:T(8,128)(2,1)} %all-gather.7.cloned.1.call-done), kind=kOutput, calls=%fused_computation.6 | convolution fusion | flops 8590983168 | bytes 27262976 | tf_op jit(solution)/shard_map/bij,bjk->bik/dot_general | solution.py:8
  673.0 0.0 all-gather.9.cloned.1.call-update
  673.0 258.1 %all-reduce.5.cloned.1.call-done = bf16[1024,4096]{1,0:T(8,128)(2,1)} async-done(((bf16[1024,4096]{1,0:T(8,128)(2,1)}), bf16[1024,4096]{1,0:T(8,128)(2,1)}) %all-reduce.5.cloned.1.call-update) | async-done | bytes 8388624 | tf_op jit(solution)/shard_map/psum | solution.py:18
  931.1 59.4 %all-gather.9.cloned.1.call-done = bf16[2,512,4096]{2,1,0:T(8,128)(2,1)} async-done(((bf16[2,512,1024]{2,1,0:T(8,128)(2,1)}), bf16[2,512,4096]{2,1,0:T(8,128)(2,1)}) %all-gather.9.cloned.1.call-update) | async-done | bytes 8388624 | tf_op jit(solution)/shard_map/all_gather | solution.py:24
  990.5 0.0 copy-start.1
  990.5 16.6 %divide_convert_fusion = (bf16[2,512,1024]{2,1,0:T(8,128)(2,1)}, bf16[2,512,1024]{2,1,0:T(8,128)(2,1)}) fusion(f32[2,512,1024]{2,1,0:T(8,128)} %param.7, bf16[2,512,4096]{2,1,0:T(8,128)(2,1)} %all-gather.9.cloned.1.call-done, bf16[1024,4096]{1,0:T(8,128)(2,1)} %all-reduce.5.cloned.1.call-done), kind=kOutput, calls=%fused_computation.4 | convolution fusion | flops 8595177472 | bytes 25165824 | tf_op jit(solution)/shard_map/bik,qk->biq/dot_general | solution.py:12
  1007.1 0.0 copy-done.1
Async XLA Ops:
  7.2 232.9 %copy-start = (bf16[2,1024,512]{2,1,0:T(8,128)(2,1)S(1)}, bf16[2,1024,512]{2,1,0:T(8,128)(2,1)}, u32[]{:S(2)}) copy-start(bf16[2,1024,512]{2,1,0:T(8,128)(2,1)} %param.9) | copy-start | bytes 6291460
  7.2 232.9 %all-gather.5.cloned.1.call-start = ((), (), s32[]{:S(2)}) async-start(), calls=%async_computation | async-start | bytes 18874368 | tf_op jit(solution)/shard_map/all_gather | solution.py:19
  7.9 266.4 %all-gather.11.cloned.1.call-start = ((), (), s32[]{:S(2)}) async-start(), calls=%async_computation.4 | async-start | bytes 5242880 | tf_op jit(solution)/shard_map/all_gather | solution.py:16
  8.7 495.1 %all-gather.7.cloned.1.call-start = ((), (), s32[]{:S(2)}) async-start(), calls=%async_computation.2 | async-start | bytes 18874368 | tf_op jit(solution)/shard_map/all_gather | solution.py:22
  9.4 647.8 %all-reduce.3.cloned.1.call-start = ((), (), s32[]{:S(2)}) async-start(), calls=%async_computation.1 | async-start | bytes 16777216 | tf_op jit(solution)/shard_map/psum | solution.py:21
  257.2 17.2 %copy-start.2 = (bf16[512,1024]{1,0:T(8,128)(2,1)S(1)}, bf16[512,1024]{1,0:T(8,128)(2,1)}, u32[]{:S(2)}) copy-start(bf16[512,1024]{1,0:T(8,128)(2,1)} %param.11) | copy-start | bytes 3145732
  257.2 673.9 %all-reduce.5.cloned.1.call-start = ((), (), s32[]{:S(2)}) async-start(), calls=%async_computation.5 | async-start | bytes 16777216 | tf_op jit(solution)/shard_map/psum | solution.py:18
  283.3 707.2 %all-gather.9.cloned.1.call-start = ((), (), s32[]{:S(2)}) async-start(), calls=%async_computation.3 | async-start | bytes 10485760 | tf_op jit(solution)/shard_map/all_gather | solution.py:24
  990.5 16.6 %copy-start.1 = (bf16[2,1024,512]{2,1,0:T(8,128)(2,1)S(1)}, bf16[2,1024,512]{2,1,0:T(8,128)(2,1)}, u32[]{:S(2)}) copy-start(bf16[2,1024,512]{2,1,0:T(8,128)(2,1)} %param.9) | copy-start | bytes 6291460
Sparse Core Ops, SparseCore 0:
  10.0 230.0 all-gather.4
  241.6 32.6 all-gather.10
  276.5 227.2 all-gather.6
  506.1 151.0 all-reduce.2
  660.9 270.1 all-reduce.4
  933.1 57.3 all-gather.8
where the time goes:
time: 1010 us
  waiting for transfers between devices  941 us (93%)
  matrix products  58.4 us (6%)
  between operations  14.1 us (1%)
    psum x1, waiting for transfers between devices, local(): right_panel = lax.psum(right_terms.astype(jnp.bfloat16), 'row')  258 us
    all_gather x1, waiting for transfers between devices, local(): old_rows = lax.all_gather(left_old, 'row', axis=2, tiled=True)  231 us
    all_gather x1, waiting for transfers between devices, local(): lax.all_gather(moment, 'row', axis=1, tiled=True)  220 us
    psum x1, waiting for transfers between devices, local(): left_panel = lax.psum(left_terms.astype(jnp.bfloat16), 'col')  153 us
    all_gather x1, waiting for transfers between devices, local(): lax.all_gather(rotated, 'col', axis=2, tiled=True)  59.4 us
  transfers between devices with their start and end apart: 6, of which 6 were waited for; matrix products, arithmetic and copies ran while one was open for 4% of the time, Pallas kernels for 0%

commit v1 on v0

--- a/solution.py
+++ b/solution.py
@@ -19,7 +19,7 @@
     old_rows = lax.all_gather(left_old, "row", axis=2, tiled=True)
     left_terms = jnp.einsum("bwi,bwj->bij", left_new, old_rows, preferred_element_type=jnp.float32)
     left_panel = lax.psum(left_terms.astype(jnp.bfloat16), "col")
-    summed = fold_stacked(left_panel, lax.all_gather(moment, "row", axis=1, tiled=True))
+    summed = fold_stacked(left_panel, jnp.concatenate(lax.all_gather(moment, "row"), axis=1))
     rotated = summed.astype(jnp.bfloat16)
     result = fold_right(right_panel, lax.all_gather(rotated, "col", axis=2, tiled=True))
     moment_new = result.astype(jnp.bfloat16)

time: 1010 us -> 1010 us (level)
  waiting for transfers between devices: 941 us -> 927 us
  local copies, waits for them, and re-layouts: 0.02 us -> 14 us
    psum x1, waiting for transfers between devices: 153 us -> 139 us  [local(): left_panel = lax.psum(left_terms.astype(jnp.bfloat16), 'col')]
    reshape x0 -> x1, local copies, waits for them, and re-layouts: none -> 13.9 us  [local(): jnp.concatenate(lax.all_gather(moment, 'row'), axis=1)]
  transfers between devices with their start and end apart: 6 -> 6, of which waited for: 6 -> 6; matrix products, arithmetic and copies ran while one was open for 4% -> 5% of each run, Pallas kernels for 0% -> 0%
where the time goes in v1:
time: 1010 us
  waiting for transfers between devices  927 us (92%)
  matrix products  58.4 us (6%)
  between operations  14.1 us (1%)
  local copies, waits for them, and re-layouts  14 us (1%)
    psum x1, waiting for transfers between devices, local(): right_panel = lax.psum(right_terms.astype(jnp.bfloat16), 'row')  258 us
    all_gather x1, waiting for transfers between devices, local(): old_rows = lax.all_gather(left_old, 'row', axis=2, tiled=True)  231 us
    all_gather x1, waiting for transfers between devices, local(): lax.all_gather(moment, 'row')  220 us
    psum x1, waiting for transfers between devices, local(): left_panel = lax.psum(left_terms.astype(jnp.bfloat16), 'col')  139 us
    all_gather x1, waiting for transfers between devices, local(): lax.all_gather(rotated, 'col', axis=2, tiled=True)  59.4 us
  transfers between devices with their start and end apart: 6, of which 6 were waited for; matrix products, arithmetic and copies ran while one was open for 5% of the time, Pallas kernels for 0%

profile of v1, /device:TPU:0, one launch (start us, length us, event | category | flops | bytes accessed | tf_op | source)
XLA Modules:
  0.0 1013.9 jit_solution(15849557869698540945)
XLA Ops:
  7.2 0.0 copy-start
  7.2 0.0 all-gather.6.cloned.1.call-start
  7.2 0.7 all-gather.6.cloned.1.call-update
  7.9 0.0 all-gather.10.cloned.1.call-start
  8.0 0.7 all-gather.10.cloned.1.call-update
  8.7 0.0 all-gather.12.cloned.1.call-start
  8.7 0.7 all-gather.12.cloned.1.call-update
  9.4 0.0 all-reduce.3.cloned.1.call-start
  9.4 230.6 %all-gather.6.cloned.1.call-done = bf16[2,1024,4096]{2,1,0:T(8,128)(2,1)} async-done(((bf16[2,1024,512]{2,1,0:T(8,128)(2,1)}), bf16[2,1024,4096]{2,1,0:T(8,128)(2,1)}) %all-gather.6.cloned.1.call-update) | async-done | bytes 16777232 | tf_op jit(solution)/shard_map/all_gather | solution.py:19
  240.1 0.0 copy-done
  240.1 17.1 %convolution_convert_fusion.1 = bf16[2,512,4096]{2,1,0:T(8,128)(2,1)} fusion(bf16[2,1024,512]{2,1,0:T(8,128)(2,1)S(1)} %copy-done, bf16[2,1024,4096]{2,1,0:T(8,128)(2,1)} %all-gather.6.cloned.1.call-done), kind=kOutput, calls=%fused_computation.3 | convolution fusion | flops 8594128896 | bytes 27262976 | tf_op jit(solution)/shard_map/bwi,bwj->bij/dot_general | solution.py:20
  257.2 0.0 copy-start.2
  257.2 0.0 all-reduce.3.cloned.1.call-update
  257.2 0.0 all-reduce.5.cloned.1.call-start
  257.3 17.1 %all-gather.10.cloned.1.call-done = bf16[512,4096]{1,0:T(8,128)(2,1)} async-done(((bf16[512,1024]{1,0:T(8,128)(2,1)}), bf16[512,4096]{1,0:T(8,128)(2,1)}) %all-gather.10.cloned.1.call-update) | async-done | bytes 4194320 | tf_op jit(solution)/shard_map/all_gather | solution.py:16
  274.3 0.0 copy-done.2
  274.3 8.9 convolution_convert_fusion
  283.3 0.0 all-reduce.5.cloned.1.call-update
  283.3 0.2 all-gather.8.cloned.1.call-start
  283.5 220.3 %all-gather.12.cloned.1.call-done = bf16[16,512,1024]{2,1,0:T(8,128)(2,1)} async-done(((bf16[2,512,1024]{2,1,0:T(8,128)(2,1)}), bf16[16,512,1024]{2,1,0:T(8,128)(2,1)}) %all-gather.12.cloned.1.call-update) | async-done | bytes 16777232 | tf_op jit(solution)/shard_map/all_gather | solution.py:22
  503.8 13.9 %copy.11 = bf16[2,8,512,1024]{3,2,1,0:T(8,128)(2,1)} copy(bf16[2,8,512,1024]{3,2,0,1:T(8,128)(2,1)} %bitcast.18) | data formatting | bytes 33554432 | tf_op jit(solution)/shard_map/reshape | solution.py:22
  517.7 139.4 %all-reduce.3.cloned.1.call-done = bf16[2,512,4096]{2,1,0:T(8,128)(2,1)} async-done(((bf16[2,512,4096]{2,1,0:T(8,128)(2,1)}), bf16[2,512,4096]{2,1,0:T(8,128)(2,1)}) %all-reduce.3.cloned.1.call-update) | async-done | bytes 8388624 | tf_op jit(solution)/shard_map/psum | solution.py:21
  657.2 15.7 %convolution_convert_fusion.2 = bf16[2,512,1024]{2,1,0:T(8,128)(2,1)} fusion(bf16[2,512,4096]{2,1,0:T(8,128)(2,1)} %all-reduce.3.cloned.1.call-done, bf16[2,4096,1024]{2,1,0:T(8,128)(2,1)} %bitcast.19), kind=kOutput, calls=%fused_computation.6 | convolution fusion | flops 8590983168 | bytes 27262976 | tf_op jit(solution)/shard_map/bij,bjk->bik/dot_general | solution.py:8
  672.9 0.0 all-gather.8.cloned.1.call-update
  672.9 258.2 %all-reduce.5.cloned.1.call-done = bf16[1024,4096]{1,0:T(8,128)(2,1)} async-done(((bf16[1024,4096]{1,0:T(8,128)(2,1)}), bf16[1024,4096]{1,0:T(8,128)(2,1)}) %all-reduce.5.cloned.1.call-update) | async-done | bytes 8388624 | tf_op jit(solution)/shard_map/psum | solution.py:18
  931.1 59.4 %all-gather.8.cloned.1.call-done = bf16[2,512,4096]{2,1,0:T(8,128)(2,1)} async-done(((bf16[2,512,1024]{2,1,0:T(8,128)(2,1)}), bf16[2,512,4096]{2,1,0:T(8,128)(2,1)}) %all-gather.8.cloned.1.call-update) | async-done | bytes 8388624 | tf_op jit(solution)/shard_map/all_gather | solution.py:24
  990.5 0.0 copy-start.1
  990.5 16.6 %divide_convert_fusion = (bf16[2,512,1024]{2,1,0:T(8,128)(2,1)}, bf16[2,512,1024]{2,1,0:T(8,128)(2,1)}) fusion(f32[2,512,1024]{2,1,0:T(8,128)} %param.7, bf16[2,512,4096]{2,1,0:T(8,128)(2,1)} %all-gather.8.cloned.1.call-done, bf16[1024,4096]{1,0:T(8,128)(2,1)} %all-reduce.5.cloned.1.call-done), kind=kOutput, calls=%fused_computation.4 | convolution fusion | flops 8595177472 | bytes 25165824 | tf_op jit(solution)/shard_map/bik,qk->biq/dot_general | solution.py:12
  1007.1 0.0 copy-done.1
Async XLA Ops:
  7.2 232.9 %copy-start = (bf16[2,1024,512]{2,1,0:T(8,128)(2,1)S(1)}, bf16[2,1024,512]{2,1,0:T(8,128)(2,1)}, u32[]{:S(2)}) copy-start(bf16[2,1024,512]{2,1,0:T(8,128)(2,1)} %param.9) | copy-start | bytes 6291460
  7.2 232.9 %all-gather.6.cloned.1.call-start = ((), (), s32[]{:S(2)}) async-start(), calls=%async_computation | async-start | bytes 18874368 | tf_op jit(solution)/shard_map/all_gather | solution.py:19
  7.9 266.4 %all-gather.10.cloned.1.call-start = ((), (), s32[]{:S(2)}) async-start(), calls=%async_computation.3 | async-start | bytes 5242880 | tf_op jit(solution)/shard_map/all_gather | solution.py:16
  8.7 495.1 %all-gather.12.cloned.1.call-start = ((), (), s32[]{:S(2)}) async-start(), calls=%async_computation.5 | async-start | bytes 18874368 | tf_op jit(solution)/shard_map/all_gather | solution.py:22
  9.4 647.8 %all-reduce.3.cloned.1.call-start = ((), (), s32[]{:S(2)}) async-start(), calls=%async_computation.1 | async-start | bytes 16777216 | tf_op jit(solution)/shard_map/psum | solution.py:21
  257.2 17.1 %copy-start.2 = (bf16[512,1024]{1,0:T(8,128)(2,1)S(1)}, bf16[512,1024]{1,0:T(8,128)(2,1)}, u32[]{:S(2)}) copy-start(bf16[512,1024]{1,0:T(8,128)(2,1)} %param.11) | copy-start | bytes 3145732
  257.2 673.9 %all-reduce.5.cloned.1.call-start = ((), (), s32[]{:S(2)}) async-start(), calls=%async_computation.4 | async-start | bytes 16777216 | tf_op jit(solution)/shard_map/psum | solution.py:18
  283.3 707.2 %all-gather.8.cloned.1.call-start = ((), (), s32[]{:S(2)}) async-start(), calls=%async_computation.2 | async-start | bytes 10485760 | tf_op jit(solution)/shard_map/all_gather | solution.py:24
  990.5 16.6 %copy-start.1 = (bf16[2,1024,512]{2,1,0:T(8,128)(2,1)S(1)}, bf16[2,1024,512]{2,1,0:T(8,128)(2,1)}, u32[]{:S(2)}) copy-start(bf16[2,1024,512]{2,1,0:T(8,128)(2,1)} %param.9) | copy-start | bytes 6291460
Sparse Core Ops, SparseCore 0:
  10.0 230.0 all-gather.5
  241.6 32.6 all-gather.9
  276.4 227.2 all-gather.11
  506.1 151.0 all-reduce.2
  660.9 270.1 all-reduce.4
  933.1 57.3 all-gather.7
